TPU v7x, 128 devices: a whole 4x4x4 slice. The times are simulated.
128 devices in a mesh: row: 8 (over x_hi, z), col: 16 (over x_lo, y, core).
Axes of the slice: x: 4 (x_hi: 2, x_lo: 2; x = x_hi * 2 + x_lo), y: 4, z: 4, core: 2. Of those that a mesh axis runs over, the one named last changes fastest.
Arguments:
- customer_inputs: bfloat16 [131072, 1024], P(('row', 'col')), may hold values from -6 to 6
- candidate_inputs: bfloat16 [131072, 1024], P(('row', 'col')), may hold values from -6 to 6
- affinity_sharpness: bfloat16 [131072], P(('row', 'col')), may hold values from 4 to 40
- correct_candidate_index: int32 [131072], P(('row', 'col')), may hold values from 0 to 8191
- customer_initial_weights: bfloat16 [1024, 512], replicated, may hold values from -0.1875 to 0.1875
- customer_final_weights: bfloat16 [512, 256], replicated, may hold values from -0.25 to 0.25
- candidate_initial_weights: bfloat16 [1024, 512], replicated, may hold values from -0.1875 to 0.1875
- candidate_final_weights: bfloat16 [512, 256], replicated, may hold values from -0.25 to 0.25
Outputs:
- loss: float32 [], replicated
- grad_user_first: float32 [1024, 512], replicated
- grad_user_second: float32 [512, 256], replicated
- grad_item_first: float32 [1024, 512], replicated
- grad_item_second: float32 [512, 256], replicated
Inputs may be any that keep to these rules, and one draw needn't show every extreme that they name: correct_candidate_index[u] indexes the items of u's group in the order of the steps.
All inputs are finite; a program needn't handle non-finite values.
Results may differ from a plain program's by a relative error of at most 0.015.
Values may be sent and summed in bfloat16 or wider, within the bound.
No kernel may reach another device: no remote copies, remote signals or barrier semaphores. Data moves between devices by JAX's collectives and lax.ppermute only.
A program may use at most 128 MiB of HBM per device.

v0:
```python
import jax
import jax.numpy as jnp
from jax import lax
from jax.sharding import PartitionSpec as P

EPS = 1e-06


def laid_out(tiles, dim):
    dims = list(tiles.shape[1:])
    dims[dim] *= tiles.shape[0]
    return jnp.moveaxis(tiles, 0, dim).reshape(dims)


def copy_for_each(value, axis):
    copies = jnp.broadcast_to(value, (lax.axis_size(axis), *value.shape))
    return lax.all_to_all(copies, axis, split_axis=0, concat_axis=0, tiled=True)


def gathered_copies(value, axis, dim):
    return laid_out(copy_for_each(value, axis), dim)


def tower_forward(feats, first, second):
    pre = jnp.dot(feats, first, preferred_element_type=jnp.float32)
    hidden = jax.nn.relu(pre).astype(jnp.bfloat16)
    out = jnp.dot(hidden, second, preferred_element_type=jnp.float32)
    inv = lax.rsqrt(jnp.mean(out * out, axis=-1, keepdims=True) + EPS)
    return ((out * inv).astype(jnp.bfloat16), (pre, hidden, out, inv))


def tower_backward(feats, second, saved, grad_vec):
    pre, hidden, out, inv = saved
    grad = grad_vec.astype(jnp.float32)
    normed = out * inv
    grad_out = (inv * (grad - normed * jnp.mean(grad * normed, axis=-1, keepdims=True))).astype(
        jnp.bfloat16
    )
    grad_second = jnp.dot(hidden.T, grad_out, preferred_element_type=jnp.float32)
    grad_hidden = jnp.dot(grad_out, second.T, preferred_element_type=jnp.float32)
    grad_pre = jnp.where(pre > 0, grad_hidden, 0.0).astype(jnp.bfloat16)
    grad_first = jnp.dot(feats.T, grad_pre, preferred_element_type=jnp.float32)
    return (grad_first, grad_second)


def positive_pair_logit(
    shopper_vector, gathered_entries, affinity_sharpness, correct_candidate_index, resident_table
):
    latent_code = shopper_vector.shape[-1]
    coolness_fp32_number = affinity_sharpness.astype(jnp.float32)
    affinity_matrix = (
        coolness_fp32_number[:, None]
        * jnp.einsum(
            "ue,ie->ui", shopper_vector, gathered_entries, preferred_element_type=jnp.float32
        )
        / latent_code
    )
    lse = jax.nn.logsumexp(affinity_matrix, axis=1)
    columns = lax.broadcasted_iota(jnp.int32, affinity_matrix.shape, 1)
    target_column = columns == correct_candidate_index[:, None]
    picked = jnp.sum(jnp.where(target_column, affinity_matrix, 0.0), axis=1)
    softmax_likelihood = jnp.exp(affinity_matrix - lse[:, None])
    sensitivity_of_affinities = (
        (softmax_likelihood - target_column.astype(jnp.float32))
        * (coolness_fp32_number / (latent_code * resident_table))[:, None]
    ).astype(jnp.bfloat16)
    customer_derivative = jnp.dot(
        sensitivity_of_affinities, gathered_entries, preferred_element_type=jnp.float32
    )
    return (lse, sensitivity_of_affinities, customer_derivative, jnp.sum(lse - picked))


def body(
    customer_inputs,
    candidate_inputs,
    affinity_sharpness,
    correct_candidate_index,
    customer_initial_weights,
    customer_final_weights,
    candidate_initial_weights,
    candidate_final_weights,
):
    resident_table = customer_inputs.shape[0]
    shopper_vector, user_saved = tower_forward(
        customer_inputs, customer_initial_weights, customer_final_weights
    )
    offered_thing_vector, item_saved = tower_forward(
        candidate_inputs, candidate_initial_weights, candidate_final_weights
    )
    latent_code = shopper_vector.shape[-1]
    gathered_entries = lax.all_gather(offered_thing_vector, "row", axis=0, tiled=True)
    lse, sensitivity_of_affinities, customer_derivative, loss_local = positive_pair_logit(
        shopper_vector,
        gathered_entries,
        affinity_sharpness,
        correct_candidate_index,
        resident_table,
    )
    all_users, all_scales = (
        lax.all_gather(shopper_vector, "row", axis=0, tiled=True),
        lax.all_gather(affinity_sharpness, "row", axis=0, tiled=True),
    )
    all_positive = gathered_copies(correct_candidate_index, "row", 0)
    all_lse = gathered_copies(lse, "row", 0)
    coolness_fp32_number = all_scales.astype(jnp.float32)
    affinity_matrix = (
        coolness_fp32_number[:, None]
        * jnp.einsum(
            "ue,ie->ui", all_users, offered_thing_vector, preferred_element_type=jnp.float32
        )
        / latent_code
    )
    start = lax.axis_index("row") * resident_table
    columns = lax.broadcasted_iota(jnp.int32, affinity_matrix.shape, 1) + start
    target_column = columns == all_positive[:, None]
    softmax_likelihood = jnp.exp(affinity_matrix - all_lse[:, None])
    group_dlogits = (
        (softmax_likelihood - target_column.astype(jnp.float32))
        * (coolness_fp32_number / (latent_code * resident_table))[:, None]
    ).astype(jnp.bfloat16)
    candidate_derivative = jnp.einsum(
        "ui,ue->ie", group_dlogits, all_users, preferred_element_type=jnp.float32
    )
    grad_user_first, grad_user_second = tower_backward(
        customer_inputs,
        customer_final_weights,
        user_saved,
        customer_derivative.astype(jnp.bfloat16),
    )
    grad_item_first, grad_item_second = tower_backward(
        candidate_inputs,
        candidate_final_weights,
        item_saved,
        candidate_derivative.astype(jnp.bfloat16),
    )
    summed = (
        lax.psum(grad_user_first.astype(jnp.bfloat16), ("row", "col")).astype(jnp.float32),
        lax.psum(grad_user_second.astype(jnp.bfloat16), ("row", "col")).astype(jnp.float32),
        lax.psum(grad_item_first.astype(jnp.bfloat16), ("row", "col")).astype(jnp.float32),
        lax.psum(grad_item_second.astype(jnp.bfloat16), ("row", "col")).astype(jnp.float32),
        lax.psum(loss_local.astype(jnp.bfloat16), ("row", "col")).astype(jnp.float32),
    )
    users_total = resident_table * lax.axis_size("row") * lax.axis_size("col")
    return (summed[4] / users_total, summed[0], summed[1], summed[2], summed[3])


def solution(mesh):
    placed = (
        P(("row", "col"), None),
        P(("row", "col"), None),
        P(("row", "col")),
        P(("row", "col")),
        P(),
        P(),
        P(),
        P(),
    )
    return jax.shard_map(
        body, mesh=mesh, in_specs=placed, out_specs=(P(), P(), P(), P(), P()), check_vma=False
    )
```

profile of v0, /device:TPU:1, one launch (start us, length us, event | category | flops | bytes accessed | tf_op | source)
XLA Modules:
  0.0 351.3 jit_solution(15818196188370760790)
XLA Ops:
  7.2 3.3 fusion.28
  10.5 1.3 copy-done.4
  12.4 0.9 multiply_convert_fusion.8
  13.3 0.6 broadcast_in_dim.15
  13.9 8.3 %all-to-all-start.1 = ((s32[8,1,1024]{2,1,0:T(1,128)}), s32[8,1,1024]{2,1,0:T(1,128)S(1)}, u32[]{:S(2)}, u32[]{:S(2)}) async-start(s32[8,1,1024]{2,1,0:T(1,128)} %broadcast_in_dim.15), calls=%async_computation.1 | async-start | bytes 65536 | tf_op jit(solution)/shard_map/all_to_all | solution.py:17
  22.3 2.5 fusion.27
  24.8 1.3 copy-done.6
  26.7 0.9 copy-done.2
  27.6 0.9 multiply_convert_fusion.9
  28.6 26.5 %all_gather.10 = bf16[8192]{0:T(1024)(128)(2,1)S(1)} all-gather(bf16[1024]{0:T(1024)(128)(2,1)S(1)} %copy-done.13), channel_id=1, replica_groups=mesh['row'=8,'col'=16] {'row'}, dimensions={0}, use_global_device_ids=true | all-gather | bytes 18432 | tf_op jit(solution)/shard_map/all_gather | solution.py:101
  55.1 32.1 %all-gather.3.cloned.1.call-done = bf16[8192,256]{0,1:T(8,128)(2,1)} async-done(((bf16[1024,256]{0,1:T(8,128)(2,1)}), bf16[8192,256]{0,1:T(8,128)(2,1)}) %all-gather.3.cloned.1.call-update) | async-done | bytes 4194320 | tf_op jit(solution)/shard_map/all_gather | solution.py:91
  87.2 16.0 %fusion = (f32[1024]{0:T(1024)S(1)}, f32[1024,8192]{1,0:T(8,128)}) fusion(f32[1024]{0:T(1024)S(1)} %convert_element_type.90, bf16[1024,256]{0,1:T(8,128)(2,1)} %multiply_convert_fusion.9, bf16[8192,256]{0,1:T(8,128)(2,1)} %all-gather.3.cloned.1.call-done), kind=kOutput, calls=%fused_computation.6 | convolution fusion | flops 4320132096 | bytes 38281216 | tf_op jit(solution)/shard_map/ue,ie->ui/dot_general | solution.py:53
  103.2 18.4 %select_reduce_fusion = (f32[1024]{0:T(1024)S(1)}, f32[1024]{0:T(1024)S(1)}) fusion(f32[1024,8192]{1,0:T(8,128)} %get-tuple-element.28, s32[1024]{0:T(1024)S(1)} %copy-done.14, f32[1024]{0:T(1024)S(1)} %convert_element_type.90, f32[1024]{0:T(1024)S(1)} %is-finite_select_fusion), kind=kLoop, calls=%fused_computation.2 | loop fusion | flops 58718208 | bytes 33574912 | tf_op jit(solution)/shard_map/reduce_sum | solution.py:61
  121.6 0.6 subtract_reduce_fusion
  122.3 20.4 %fusion.9 = (f32[1024]{0:T(1024)S(1)}, bf16[1024,256]{0,1:T(8,128)(2,1)S(1)}) fusion(f32[1024,256]{0,1:T(8,128)S(1)} %copy-done.3, f32[1024]{0:T(1024)S(1)} %add_rsqrt_fusion.1, bf16[8192,256]{0,1:T(8,128)(2,1)} %all-gather.3.cloned.1.call-done, f32[1024,8192]{1,0:T(8,128)} %get-tuple-element.28, f32[1024]{0:T(1024)S(1)} %broadcast_multiply_fusion.1, ...), kind=kOutput, calls=%fused_computation.26 | convolution fusion | flops 4363385856 | bytes 39346176 | tf_op jit(solution)/shard_map/dot_general | solution.py:67
  142.6 1.0 fusion.11
  143.6 4.4 %fusion.5 = bf16[1024,512]{0,1:T(8,128)(2,1)} fusion(bf16[1024,1024]{1,0:T(8,128)(2,1)S(1)} %copy-done, f32[1024,512]{1,0:T(8,128)} %copy-done.6, bf16[1024,256]{0,1:T(8,128)(2,1)} %fusion.11, bf16[512,256]{1,0:T(8,128)(2,1)S(1)} %copy-done.10), kind=kOutput, calls=%fused_computation.16 | convolution fusion | flops 1344274432 | bytes 6029312 | tf_op jit(solution)/shard_map/dot_general | solution.py:42
  148.0 0.6 broadcast_in_dim.14
  148.6 3.3 all-to-all-start
  152.0 2.9 convolution_convert_fusion.3
  154.9 4.5 %all-gather.5.cloned.1.call-done = bf16[8192,256]{0,1:T(8,128)(2,1)} async-done(((bf16[1024,256]{0,1:T(8,128)(2,1)}), bf16[8192,256]{0,1:T(8,128)(2,1)}) %all-gather.5.cloned.1.call-update) | async-done | bytes 4194320 | tf_op jit(solution)/shard_map/all_gather | solution.py:100
  159.4 14.2 %multiply_convert_fusion.5.clone.4 = bf16[8192,1024]{1,0:T(8,128)(2,1)S(1)} fusion(f32[8192]{0:T(1024)S(1)} %broadcast_multiply_fusion, s32[1024]{0:T(1024)S(1)} %iota_add_fusion, f32[8192]{0:T(1024)S(1)} %bitcast.31, f32[8192]{0:T(1024)S(1)} %convert_element_type.108, s32[8192]{0:T(1024)S(1)} %bitcast.30, ...), kind=kOutput, calls=%fused_computation.clone.clone.clone.clone.clone.clone.1 | convolution fusion | flops 4362600448 | bytes 22159360 | tf_op jit(solution)/shard_map/ue,ie->ui/dot_general | solution.py:108
  173.7 4.7 %fusion.12 = (f32[1024]{0:T(1024)S(1)}, bf16[1024,256]{0,1:T(8,128)(2,1)S(1)}) fusion(f32[1024,256]{0,1:T(8,128)S(1)} %get-tuple-element.26, f32[1024]{0:T(1024)S(1)} %add_rsqrt_fusion, bf16[8192,256]{0,1:T(8,128)(2,1)S(1)} %copy-done.15, bf16[8192,1024]{1,0:T(8,128)(2,1)S(1)} %multiply_convert_fusion.5.clone.4), kind=kOutput, calls=%fused_computation.29 | convolution fusion | flops 4296276992 | bytes 22552576 | tf_op jit(solution)/shard_map/ui,ue->ie/dot_general | solution.py:121
  178.3 1.0 fusion.14
  179.3 4.4 %fusion.6 = bf16[1024,512]{0,1:T(8,128)(2,1)} fusion(bf16[1024,1024]{1,0:T(8,128)(2,1)} %param.9, f32[1024,512]{1,0:T(8,128)S(1)} %copy-done.5, bf16[1024,256]{0,1:T(8,128)(2,1)} %fusion.14, bf16[512,256]{1,0:T(8,128)(2,1)S(1)} %copy-done.12), kind=kOutput, calls=%fused_computation.17 | convolution fusion | flops 1344274432 | bytes 6029312 | tf_op jit(solution)/shard_map/dot_general | solution.py:42
  183.7 1.2 convolution_convert_fusion.2
  185.0 64.6 %psum.35 = bf16[]{:T(256)} all-reduce(bf16[]{:T(256)} %get-tuple-element.21), channel_id=1, replica_groups=mesh['row'=8,'col'=16] {'row','col'}, use_global_device_ids=true, to_apply=%region_6.7 | all-reduce | flops 1 | bytes 4 | tf_op jit(solution)/shard_map/psum | solution.py:141
  250.2 86.5 %all-reduce.3.cloned.1.call-done = (bf16[1024,512]{0,1:T(8,128)(2,1)}, bf16[1024,512]{0,1:T(8,128)(2,1)}, bf16[512,256]{1,0:T(8,128)(2,1)}, bf16[512,256]{1,0:T(8,128)(2,1)}) async-done(((bf16[1024,512]{0,1:T(8,128)(2,1)}, bf16[1024,512]{0,1:T(8,128)(2,1)}, bf16[512,256]{1,0:T(8,128)(2,1)}, bf16[512,256]{1,0:T(8,128)(2,1)}), (bf16[1024,512]{0,1:T(8,128)(2,1)}, bf16[1024,512]{0,1:T(8,128)(2,1)}, ...) | async-done | bytes 2621456 | tf_op jit(solution)/shard_map/psum | solution.py:137
  336.8 2.7 copy.15
  339.5 1.8 convert_element_type.107
  341.2 1.6 copy.16
  342.8 0.8 convert_element_type.119
  (49 shorter events, 1.3 us)
Async XLA Ops:
  7.2 15.1 %copy-start = (bf16[1024,1024]{1,0:T(8,128)(2,1)S(1)}, bf16[1024,1024]{1,0:T(8,128)(2,1)}, u32[]{:S(2)}) copy-start(bf16[1024,1024]{1,0:T(8,128)(2,1)} %param.8) | copy-start | bytes 6291460
  7.2 4.7 %copy-start.11 = (bf16[512,256]{1,0:T(8,128)(2,1)S(1)}, bf16[512,256]{1,0:T(8,128)(2,1)}, u32[]{:S(2)}) copy-start(bf16[512,256]{1,0:T(8,128)(2,1)} %param.15) | copy-start | bytes 786436
  7.2 80.0 %all-gather.3.cloned.1.call-start = ((), (), s32[]{:S(2)}) async-start(), calls=%async_computation.2 | async-start | bytes 4718592 | tf_op jit(solution)/shard_map/all_gather | solution.py:91
  10.5 1.3 copy-start.4
  11.8 1.4 copy-start.14
  13.9 134.1 %all-to-all-start.1 = ((s32[8,1,1024]{2,1,0:T(1,128)}), s32[8,1,1024]{2,1,0:T(1,128)S(1)}, u32[]{:S(2)}, u32[]{:S(2)}) async-start(s32[8,1,1024]{2,1,0:T(1,128)} %broadcast_in_dim.15), calls=%async_computation.1 | async-start | bytes 65536 | tf_op jit(solution)/shard_map/all_to_all | solution.py:17
  22.2 3.9 %copy-start.10 = (bf16[512,256]{1,0:T(8,128)(2,1)S(1)}, bf16[512,256]{1,0:T(8,128)(2,1)}, u32[]{:S(2)}) copy-start(bf16[512,256]{1,0:T(8,128)(2,1)} %param.13) | copy-start | bytes 786436
  22.2 137.2 %all-gather.5.cloned.1.call-start = ((), (), s32[]{:S(2)}) async-start(), calls=%async_computation.3 | async-start | bytes 4718592 | tf_op jit(solution)/shard_map/all_gather | solution.py:100
  24.8 1.3 copy-start.6
  26.1 2.4 copy-start.13
  26.6 1.0 copy-start.2
  103.2 19.0 %copy-start.3 = (f32[1024,256]{0,1:T(8,128)S(1)}, f32[1024,256]{0,1:T(8,128)}, u32[]{:S(2)}) copy-start(f32[1024,256]{0,1:T(8,128)} %copy-done.2) | copy-start | bytes 3145732
  148.6 10.8 %all-to-all-start = ((f32[8,1,1024]{2,1,0:T(1,128)}), f32[8,1,1024]{2,1,0:T(1,128)S(1)}, u32[]{:S(2)}, u32[]{:S(2)}) async-start(f32[8,1,1024]{2,1,0:T(1,128)} %broadcast_in_dim.14), calls=%async_computation | async-start | bytes 65536 | tf_op jit(solution)/shard_map/all_to_all | solution.py:17
  152.0 184.8 %all-reduce.3.cloned.1.call-start = ((), (), s32[]{:S(2)}) async-start(), calls=%async_computation.4 | async-start | bytes 5242880 | tf_op jit(solution)/shard_map/psum | solution.py:137
  159.4 14.2 %copy-start.15 = (bf16[8192,256]{0,1:T(8,128)(2,1)S(1)}, bf16[8192,256]{0,1:T(8,128)(2,1)}, u32[]{:S(2)}) copy-start(bf16[8192,256]{0,1:T(8,128)(2,1)} %all-gather.5.cloned.1.call-done) | copy-start | bytes 12582916
  173.6 5.7 %copy-start.5 = (f32[1024,512]{1,0:T(8,128)S(1)}, f32[1024,512]{1,0:T(8,128)}, u32[]{:S(2)}) copy-start(f32[1024,512]{1,0:T(8,128)} %copy-done.4) | copy-start | bytes 6291460
  173.6 5.7 %copy-start.12 = (bf16[512,256]{1,0:T(8,128)(2,1)S(1)}, bf16[512,256]{1,0:T(8,128)(2,1)}, u32[]{:S(2)}) copy-start(bf16[512,256]{1,0:T(8,128)(2,1)} %param.15) | copy-start | bytes 786436
  179.3 4.4 %copy-start.7 = (bf16[1024,256]{0,1:T(8,128)(2,1)S(1)}, bf16[1024,256]{0,1:T(8,128)(2,1)}, u32[]{:S(2)}) copy-start(bf16[1024,256]{0,1:T(8,128)(2,1)} %fusion.14) | copy-start | bytes 1572868
  185.0 158.7 %copy-start.1 = (bf16[1024,1024]{1,0:T(8,128)(2,1)S(1)}, bf16[1024,1024]{1,0:T(8,128)(2,1)}, u32[]{:S(2)}) copy-start(bf16[1024,1024]{1,0:T(8,128)(2,1)} %param.8) | copy-start | bytes 6291460
  336.8 4.5 %copy-start.8 = (bf16[1024,512]{0,1:T(8,128)(2,1)S(1)}, bf16[1024,512]{0,1:T(8,128)(2,1)}, u32[]{:S(2)}) copy-start(bf16[1024,512]{0,1:T(8,128)(2,1)} %get-tuple-element.18) | copy-start | bytes 3145732
  336.8 6.1 %copy-start.9 = (bf16[512,256]{1,0:T(8,128)(2,1)S(1)}, bf16[512,256]{1,0:T(8,128)(2,1)}, u32[]{:S(2)}) copy-start(bf16[512,256]{1,0:T(8,128)(2,1)} %get-tuple-element.20) | copy-start | bytes 786436
Sparse Core Ops, SparseCore 0:
  13.4 73.7 all-gather.2
  90.1 69.2 all-gather.4
  185.1 151.6 all-reduce.2
where the time goes:
time: 352 us; the launch traced here: 351 us
  waiting for transfers between devices  123 us (35%)
  blocking collectives  91.1 us (26%)
  matrix products  74.8 us (21%)
  other arithmetic  25.5 us (7%)
  between operations  15.8 us (4%)
  starting transfers between devices  11.8 us (3%)
  local copies, waits for them, and re-layouts  9.18 us (3%)
    psum x1, waiting for transfers between devices, body(): lax.psum(grad_user_first.astype(jnp.bfloat16), ('row', 'col'))  86.5 us
    psum x1, blocking collectives, body(): lax.psum(loss_local.astype(jnp.bfloat16), ('row', 'col'))  64.6 us
    all_gather x1, waiting for transfers between devices, body(): lax.all_gather(offered_thing_vector, 'row', axis=0, tiled=True)  32.1 us
    all_gather x1, blocking collectives, body(): lax.all_gather(affinity_sharpness, 'row', axis=0, tiled=True)  26.5 us
    dot_general x1, matrix products, positive_pair_logit(): jnp.dot(sensitivity_of_affinities, gathered_entries, preferred_element_ty...  20.4 us
    reduce_sum x1, other arithmetic, positive_pair_logit(): picked = jnp.sum(jnp.where(target_column, affinity_matrix, 0.0), axis=1)  18.4 us
    dot_general x1, matrix products, positive_pair_logit(): jnp.einsum('ue,ie->ui', shopper_vector, gathered_entries, preferred_eleme...  16 us
    dot_general x1, matrix products, body(): jnp.einsum('ue,ie->ui', all_users, offered_thing_vector, preferred_elemen...  14.2 us
  transfers between devices with their start and end apart: 5, of which 3 were waited for; matrix products, arithmetic and copies ran while one was open for 20% of the time, Pallas kernels for 0%

commit v1 on v0

--- a/solution.py
+++ b/solution.py
@@ -4,6 +4,11 @@
 from jax.sharding import PartitionSpec as P
 
 EPS = 1e-06
+
+
+def gather_over(x, axis, d):
+    sent = jnp.stack([x] * lax.axis_size(axis))
+    return jnp.concatenate(lax.all_to_all(sent, axis, 0, 0), axis=d)
 
 
 def laid_out(tiles, dim):
@@ -88,7 +93,7 @@
         candidate_inputs, candidate_initial_weights, candidate_final_weights
     )
     latent_code = shopper_vector.shape[-1]
-    gathered_entries = lax.all_gather(offered_thing_vector, "row", axis=0, tiled=True)
+    gathered_entries = gather_over(offered_thing_vector, "row", 0)
     lse, sensitivity_of_affinities, customer_derivative, loss_local = positive_pair_logit(
         shopper_vector,
         gathered_entries,

time: 352 us -> 380 us (1.080)
  blocking collectives: 91.1 us -> 140 us
  waiting for transfers between devices: 123 us -> 89.9 us
  starting transfers between devices: 11.8 us -> 18.5 us
  local copies, waits for them, and re-layouts: 9.18 us -> 14.4 us
    all_gather x1, blocking collectives: 26.5 us -> 69.9 us  [body(): lax.all_gather(affinity_sharpness, 'row', axis=0, tiled=True)]
    all_gather x1 -> x0, waiting for transfers between devices: 32.1 us -> none  [body(): lax.all_gather(offered_thing_vector, 'row', axis=0, tiled=True)]
    all_to_all x0 -> x1, starting transfers between devices: none -> 8.31 us  [gather_over(): return jnp.concatenate(lax.all_to_all(sent, axis, 0, 0), axis=d)]
    psum x1, blocking collectives: 64.6 us -> 69.8 us  [body(): lax.psum(loss_local.astype(jnp.bfloat16), ('row', 'col'))]
    all_gather x1, waiting for transfers between devices: 4.51 us -> 0.01 us  [body(): lax.all_gather(shopper_vector, 'row', axis=0, tiled=True)]
  transfers between devices with their start and end apart: 5 -> 5, of which waited for: 3 -> 2; matrix products, arithmetic and copies ran while one was open for 20% -> 18% of each run, Pallas kernels for 0% -> 0%
where the time goes in v1:
time: 380 us; the launch traced here: 379 us
  blocking collectives  140 us (37%)
  waiting for transfers between devices  89.9 us (24%)
  matrix products  74.8 us (20%)
  other arithmetic  25.4 us (7%)
  starting transfers between devices  18.5 us (5%)
  between operations  16.1 us (4%)
  local copies, waits for them, and re-layouts  14.4 us (4%)
    psum x1, waiting for transfers between devices, body(): lax.psum(grad_user_first.astype(jnp.bfloat16), ('row', 'col'))  86.4 us
    all_gather x1, blocking collectives, body(): lax.all_gather(affinity_sharpness, 'row', axis=0, tiled=True)  69.9 us
    psum x1, blocking collectives, body(): lax.psum(loss_local.astype(jnp.bfloat16), ('row', 'col'))  69.8 us
    dot_general x1, matrix products, positive_pair_logit(): jnp.dot(sensitivity_of_affinities, gathered_entries, preferred_element_ty...  19.8 us
    reduce_sum x1, other arithmetic, positive_pair_logit(): picked = jnp.sum(jnp.where(target_column, affinity_matrix, 0.0), axis=1)  18.4 us
    dot_general x1, matrix products, positive_pair_logit(): jnp.einsum('ue,ie->ui', shopper_vector, gathered_entries, preferred_eleme...  16.9 us
    dot_general x1, matrix products, body(): jnp.einsum('ue,ie->ui', all_users, offered_thing_vector, preferred_elemen...  14.1 us
    all_to_all x2, starting transfers between devices, copy_for_each(): return lax.all_to_all(copies, axis, split_axis=0, concat_axis=0, tiled=True)  9.91 us
  transfers between devices with their start and end apart: 5, of which 2 were waited for; matrix products, arithmetic and copies ran while one was open for 18% of the time, Pallas kernels for 0%

profile of v1, /device:TPU:1, one launch (start us, length us, event | category | flops | bytes accessed | tf_op | source)
XLA Modules:
  0.0 378.8 jit_solution(12852185114188374621)
XLA Ops:
  7.2 3.3 fusion.28
  10.5 1.3 copy-done.4
  12.3 0.9 multiply_convert_fusion.8
  13.2 2.0 copy.16
  15.2 3.3 stack.2
  18.5 8.3 %all-to-all-start = ((bf16[8,1024,256]{2,1,0:T(8,128)(2,1)}), bf16[8,1024,256]{2,1,0:T(8,128)(2,1)}, u32[]{:S(2)}, u32[]{:S(2)}) async-start(bf16[8,1024,256]{2,1,0:T(8,128)(2,1)} %stack.2), calls=%async_computation | async-start | bytes 8388608 | tf_op jit(solution)/shard_map/all_to_all | solution.py:11
  26.9 2.5 fusion.27
  29.4 1.3 copy-done.6
  31.2 0.9 copy-done.2
  32.2 0.9 multiply_convert_fusion.9
  33.1 69.9 %all_gather.6 = bf16[8192]{0:T(1024)(128)(2,1)S(1)} all-gather(bf16[1024]{0:T(1024)(128)(2,1)S(1)} %copy-done.13), channel_id=1, replica_groups=mesh['row'=8,'col'=16] {'row'}, dimensions={0}, use_global_device_ids=true | all-gather | bytes 18432 | tf_op jit(solution)/shard_map/all_gather | solution.py:106
  103.0 0.6 broadcast_in_dim.15
  103.7 3.5 all-to-all-start.2
  107.2 16.9 %fusion = (f32[1024]{0:T(1024)S(1)}, f32[1024,8192]{1,0:T(8,128)}) fusion(f32[1024]{0:T(1024)S(1)} %convert_element_type.90, bf16[1024,256]{0,1:T(8,128)(2,1)} %multiply_convert_fusion.9, bf16[8192,256]{1,0:T(8,128)(2,1)} %bitcast), kind=kOutput, calls=%fused_computation.6 | convolution fusion | flops 4320132096 | bytes 38281216 | tf_op jit(solution)/shard_map/ue,ie->ui/dot_general | solution.py:58
  124.0 18.4 %select_reduce_fusion = (f32[1024]{0:T(1024)S(1)}, f32[1024]{0:T(1024)S(1)}) fusion(f32[1024,8192]{1,0:T(8,128)} %get-tuple-element.28, s32[1024]{0:T(1024)S(1)} %copy-done.14, f32[1024]{0:T(1024)S(1)} %convert_element_type.90, f32[1024]{0:T(1024)S(1)} %is-finite_select_fusion), kind=kLoop, calls=%fused_computation.2 | loop fusion | flops 58718208 | bytes 33574912 | tf_op jit(solution)/shard_map/reduce_sum | solution.py:66
  143.0 19.8 %fusion.9 = (f32[1024]{0:T(1024)S(1)}, bf16[1024,256]{0,1:T(8,128)(2,1)S(1)}) fusion(f32[1024,256]{0,1:T(8,128)S(1)} %copy-done.3, f32[1024]{0:T(1024)S(1)} %add_rsqrt_fusion.1, bf16[8192,256]{1,0:T(8,128)(2,1)} %bitcast, f32[1024,8192]{1,0:T(8,128)} %get-tuple-element.28, f32[1024]{0:T(1024)S(1)} %broadcast_multiply_fusion.1, ...), kind=kOutput, calls=%fused_computation.26 | convolution fusion | flops 4363385856 | bytes 39346176 | tf_op jit(solution)/shard_map/dot_general | solution.py:72
  162.8 1.0 fusion.11
  163.8 4.3 %fusion.5 = bf16[1024,512]{0,1:T(8,128)(2,1)} fusion(bf16[1024,1024]{1,0:T(8,128)(2,1)S(1)} %copy-done, f32[1024,512]{1,0:T(8,128)} %copy-done.6, bf16[1024,256]{0,1:T(8,128)(2,1)} %fusion.11, bf16[512,256]{1,0:T(8,128)(2,1)S(1)} %copy-done.10), kind=kOutput, calls=%fused_computation.16 | convolution fusion | flops 1344274432 | bytes 6029312 | tf_op jit(solution)/shard_map/dot_general | solution.py:47
  168.8 6.4 %all-to-all-start.1 = ((f32[8,1,1024]{2,1,0:T(1,128)}), f32[8,1,1024]{2,1,0:T(1,128)S(1)}, u32[]{:S(2)}, u32[]{:S(2)}) async-start(f32[8,1,1024]{2,1,0:T(1,128)} %broadcast_in_dim.14), calls=%async_computation.1 | async-start | bytes 65536 | tf_op jit(solution)/shard_map/all_to_all | solution.py:22
  175.5 2.9 convolution_convert_fusion.3
  178.3 3.5 all-to-all-done.1
  181.8 14.1 %multiply_convert_fusion.5.clone.4 = bf16[8192,1024]{1,0:T(8,128)(2,1)S(1)} fusion(f32[8192]{0:T(1024)S(1)} %broadcast_multiply_fusion, s32[1024]{0:T(1024)S(1)} %iota_add_fusion, f32[8192]{0:T(1024)S(1)} %bitcast.32, f32[8192]{0:T(1024)S(1)} %convert_element_type.108, s32[8192]{0:T(1024)S(1)} %bitcast.31, ...), kind=kOutput, calls=%fused_computation.clone.clone.clone.clone.clone.clone.1 | convolution fusion | flops 4362600448 | bytes 22159360 | tf_op jit(solution)/shard_map/ue,ie->ui/dot_general | solution.py:113
  196.0 4.5 %fusion.12 = (f32[1024]{0:T(1024)S(1)}, bf16[1024,256]{0,1:T(8,128)(2,1)S(1)}) fusion(f32[1024,256]{0,1:T(8,128)S(1)} %get-tuple-element.26, f32[1024]{0:T(1024)S(1)} %add_rsqrt_fusion, bf16[8192,256]{0,1:T(8,128)(2,1)S(1)} %copy-done.15, bf16[8192,1024]{1,0:T(8,128)(2,1)S(1)} %multiply_convert_fusion.5.clone.4), kind=kOutput, calls=%fused_computation.29 | convolution fusion | flops 4296276992 | bytes 22552576 | tf_op jit(solution)/shard_map/ui,ue->ie/dot_general | solution.py:126
  200.5 1.0 fusion.14
  201.5 4.4 %fusion.6 = bf16[1024,512]{0,1:T(8,128)(2,1)} fusion(bf16[1024,1024]{1,0:T(8,128)(2,1)} %param.9, f32[1024,512]{1,0:T(8,128)S(1)} %copy-done.5, bf16[1024,256]{0,1:T(8,128)(2,1)} %fusion.14, bf16[512,256]{1,0:T(8,128)(2,1)S(1)} %copy-done.12), kind=kOutput, calls=%fused_computation.17 | convolution fusion | flops 1344274432 | bytes 6029312 | tf_op jit(solution)/shard_map/dot_general | solution.py:47
  205.9 1.2 convolution_convert_fusion.2
  207.1 69.8 %psum.35 = bf16[]{:T(256)} all-reduce(bf16[]{:T(256)} %get-tuple-element.21), channel_id=1, replica_groups=mesh['row'=8,'col'=16] {'row','col'}, use_global_device_ids=true, to_apply=%region_6.7 | all-reduce | flops 1 | bytes 4 | tf_op jit(solution)/shard_map/psum | solution.py:146
  277.5 86.4 %all-reduce.3.cloned.1.call-done = (bf16[1024,512]{0,1:T(8,128)(2,1)}, bf16[1024,512]{0,1:T(8,128)(2,1)}, bf16[512,256]{1,0:T(8,128)(2,1)}, bf16[512,256]{1,0:T(8,128)(2,1)}) async-done(((bf16[1024,512]{0,1:T(8,128)(2,1)}, bf16[1024,512]{0,1:T(8,128)(2,1)}, bf16[512,256]{1,0:T(8,128)(2,1)}, bf16[512,256]{1,0:T(8,128)(2,1)}), (bf16[1024,512]{0,1:T(8,128)(2,1)}, bf16[1024,512]{0,1:T(8,128)(2,1)}, ...) | async-done | bytes 2621456 | tf_op jit(solution)/shard_map/psum | solution.py:142
  364.0 2.7 copy.17
  366.6 1.8 convert_element_type.107
  368.4 1.6 copy.18
  370.0 0.8 convert_element_type.119
  (50 shorter events, 2.7 us)
Async XLA Ops:
  7.2 19.7 %copy-start = (bf16[1024,1024]{1,0:T(8,128)(2,1)S(1)}, bf16[1024,1024]{1,0:T(8,128)(2,1)}, u32[]{:S(2)}) copy-start(bf16[1024,1024]{1,0:T(8,128)(2,1)} %param.8) | copy-start | bytes 6291460
  7.2 4.6 %copy-start.11 = (bf16[512,256]{1,0:T(8,128)(2,1)S(1)}, bf16[512,256]{1,0:T(8,128)(2,1)}, u32[]{:S(2)}) copy-start(bf16[512,256]{1,0:T(8,128)(2,1)} %param.15) | copy-start | bytes 786436
  10.5 1.3 copy-start.4
  18.5 84.5 %all-to-all-start = ((bf16[8,1024,256]{2,1,0:T(8,128)(2,1)}), bf16[8,1024,256]{2,1,0:T(8,128)(2,1)}, u32[]{:S(2)}, u32[]{:S(2)}) async-start(bf16[8,1024,256]{2,1,0:T(8,128)(2,1)} %stack.2), calls=%async_computation | async-start | bytes 8388608 | tf_op jit(solution)/shard_map/all_to_all | solution.py:11
  26.8 3.9 %copy-start.10 = (bf16[512,256]{1,0:T(8,128)(2,1)S(1)}, bf16[512,256]{1,0:T(8,128)(2,1)}, u32[]{:S(2)}) copy-start(bf16[512,256]{1,0:T(8,128)(2,1)} %param.13) | copy-start | bytes 786436
  26.8 155.0 %all-gather.2.cloned.1.call-start = ((), (), s32[]{:S(2)}) async-start(), calls=%async_computation.3 | async-start | bytes 4718592 | tf_op jit(solution)/shard_map/all_gather | solution.py:105
  29.4 1.3 copy-start.6
  30.7 2.4 copy-start.13
  30.7 72.4 %copy-start.14 = (s32[1024]{0:T(1024)S(1)}, s32[1024]{0:T(1024)}, u32[]{:S(2)}) copy-start(s32[1024]{0:T(1024)} %param.11) | copy-start | bytes 12292
  31.2 1.0 copy-start.2
  103.7 64.5 %all-to-all-start.2 = ((s32[8,1,1024]{2,1,0:T(1,128)}), s32[8,1,1024]{2,1,0:T(1,128)S(1)}, u32[]{:S(2)}, u32[]{:S(2)}) async-start(s32[8,1,1024]{2,1,0:T(1,128)} %broadcast_in_dim.15), calls=%async_computation.2 | async-start | bytes 65536 | tf_op jit(solution)/shard_map/all_to_all | solution.py:22
  124.0 19.0 %copy-start.3 = (f32[1024,256]{0,1:T(8,128)S(1)}, f32[1024,256]{0,1:T(8,128)}, u32[]{:S(2)}) copy-start(f32[1024,256]{0,1:T(8,128)} %copy-done.2) | copy-start | bytes 3145732
  168.8 13.0 %all-to-all-start.1 = ((f32[8,1,1024]{2,1,0:T(1,128)}), f32[8,1,1024]{2,1,0:T(1,128)S(1)}, u32[]{:S(2)}, u32[]{:S(2)}) async-start(f32[8,1,1024]{2,1,0:T(1,128)} %broadcast_in_dim.14), calls=%async_computation.1 | async-start | bytes 65536 | tf_op jit(solution)/shard_map/all_to_all | solution.py:22
  175.2 188.7 %all-reduce.3.cloned.1.call-start = ((), (), s32[]{:S(2)}) async-start(), calls=%async_computation.4 | async-start | bytes 5242880 | tf_op jit(solution)/shard_map/psum | solution.py:142
  181.8 14.1 %copy-start.15 = (bf16[8192,256]{0,1:T(8,128)(2,1)S(1)}, bf16[8192,256]{0,1:T(8,128)(2,1)}, u32[]{:S(2)}) copy-start(bf16[8192,256]{0,1:T(8,128)(2,1)} %all-gather.2.cloned.1.call-done) | copy-start | bytes 12582916
  196.0 5.5 %copy-start.5 = (f32[1024,512]{1,0:T(8,128)S(1)}, f32[1024,512]{1,0:T(8,128)}, u32[]{:S(2)}) copy-start(f32[1024,512]{1,0:T(8,128)} %copy-done.4) | copy-start | bytes 6291460
  196.0 5.5 %copy-start.12 = (bf16[512,256]{1,0:T(8,128)(2,1)S(1)}, bf16[512,256]{1,0:T(8,128)(2,1)}, u32[]{:S(2)}) copy-start(bf16[512,256]{1,0:T(8,128)(2,1)} %param.15) | copy-start | bytes 786436
  201.5 4.4 %copy-start.7 = (bf16[1024,256]{0,1:T(8,128)(2,1)S(1)}, bf16[1024,256]{0,1:T(8,128)(2,1)}, u32[]{:S(2)}) copy-start(bf16[1024,256]{0,1:T(8,128)(2,1)} %fusion.14) | copy-start | bytes 1572868
  207.1 163.7 %copy-start.1 = (bf16[1024,1024]{1,0:T(8,128)(2,1)S(1)}, bf16[1024,1024]{1,0:T(8,128)(2,1)}, u32[]{:S(2)}) copy-start(bf16[1024,1024]{1,0:T(8,128)(2,1)} %param.8) | copy-start | bytes 6291460
  363.9 4.5 %copy-start.8 = (bf16[1024,512]{0,1:T(8,128)(2,1)S(1)}, bf16[1024,512]{0,1:T(8,128)(2,1)}, u32[]{:S(2)}) copy-start(bf16[1024,512]{0,1:T(8,128)(2,1)} %get-tuple-element.18) | copy-start | bytes 3145732
  364.0 6.1 %copy-start.9 = (bf16[512,256]{1,0:T(8,128)(2,1)S(1)}, bf16[512,256]{1,0:T(8,128)(2,1)}, u32[]{:S(2)}) copy-start(bf16[512,256]{1,0:T(8,128)(2,1)} %get-tuple-element.20) | copy-start | bytes 786436
Sparse Core Ops, SparseCore 0:
  33.2 95.6 all-gather.1
  207.2 156.6 all-reduce.2
